TPU v7x, 32 devices: a whole 2x2x4 slice. The times are simulated.
32 devices in a mesh: dp: 8 (over z, core), tp: 4 (over y, x).
Axes of the slice: x: 2, y: 2, z: 4, core: 2. Of those that a mesh axis runs over, the one named last changes fastest.
Arguments:
- tokens: bfloat16 [4096, 4096], P('dp'), may hold values from -6 to 6
- gain: float32 [4096], replicated, may hold values from 0.1 to 1.9
- router: float32 [4096, 8], replicated, may hold values from -0.09375 to 0.09375
- routes: int32 [4096, 2], P('dp'), may hold values from 0 to 7, all different within a row
- w_gate: bfloat16 [2, 4096, 1024], P(None, 'dp', 'tp'), may hold values from -0.125 to 0.125
- w_up: bfloat16 [2, 4096, 1024], P(None, 'dp', 'tp'), may hold values from -0.125 to 0.125
- w_down: bfloat16 [2, 1024, 4096], P(None, 'dp', 'tp'), may hold values from -0.25 to 0.25
Outputs:
- mixed: bfloat16 [4096, 4096], P('dp', 'tp')
Inputs may be any that keep to these rules, and one draw needn't show every extreme that they name: `routes`: each row names two different experts.
All inputs are finite; a program needn't handle non-finite values.
Results may differ from a plain program's by a relative error of at most 0.0065.
Values may be sent and summed in bfloat16 or wider, within the bound.
A program may use at most 64 MiB of HBM per device.

v0:
```python
import jax
import jax.numpy as jnp
from jax import lax
from jax.sharding import PartitionSpec as P

EPS = 1e-06
ROUTE_SCALE = 2.5


def per_device(tokens, gain, router, routes, w_gate, w_up, w_down):
    values = tokens.astype(jnp.float32)
    square = jnp.mean(values * values, axis=-1, keepdims=True)
    normed = (values * lax.rsqrt(square + EPS) * gain).astype(jnp.bfloat16)
    scores = jax.nn.sigmoid(
        jnp.dot(normed.astype(jnp.float32), router, precision=lax.Precision.HIGHEST)
    )
    labels = jnp.arange(router.shape[1], dtype=jnp.int32)
    picked_mask = (routes[:, :, None] == labels[None, None, :]).astype(jnp.float32)
    picked = jnp.sum(picked_mask * scores[:, None, :], axis=-1)
    chosen = jnp.sum(picked_mask, axis=1)
    combine = chosen * scores * ROUTE_SCALE / jnp.sum(picked, axis=-1, keepdims=True)
    held_weights = combine[:, : w_gate.shape[0]]
    full_gate, full_up, full_down = (
        lax.all_gather(w_gate, "dp", axis=1, tiled=True),
        lax.all_gather(w_up, "dp", axis=1, tiled=True),
        lax.all_gather(w_down, "dp", axis=1, tiled=True),
    )
    gate_value = jnp.einsum("td,edf->tef", normed, full_gate, preferred_element_type=jnp.float32)
    up_value = jnp.einsum("td,edf->tef", normed, full_up, preferred_element_type=jnp.float32)
    hidden = (jax.nn.silu(gate_value) * up_value * held_weights[:, :, None]).astype(jnp.bfloat16)
    whole_hidden = lax.all_gather(hidden, "tp", axis=2, tiled=True)
    mixed = jnp.einsum("tef,efd->td", whole_hidden, full_down, preferred_element_type=jnp.float32)
    return mixed.astype(jnp.bfloat16)


def solution(mesh):
    return jax.shard_map(
        per_device,
        mesh=mesh,
        in_specs=(
            P("dp", None),
            P(),
            P(),
            P("dp", None),
            P(None, "dp", "tp"),
            P(None, "dp", "tp"),
            P(None, "dp", "tp"),
        ),
        out_specs=P("dp", "tp"),
        check_vma=False,
    )
```

profile of v0, /device:TPU:0, one launch (start us, length us, event | category | flops | bytes accessed | tf_op | source)
XLA Modules:
  0.0 201.4 jit_solution(2412415738272658088)
XLA Ops:
  6.5 0.0 copy-start
  6.5 0.0 copy-start.3
  6.5 0.0 all-gather.5.cloned.1.call-start
  6.5 0.7 all-gather.5.cloned.1.call-update
  7.3 0.0 all-gather.7.cloned.1.call-start
  7.3 0.7 all-gather.7.cloned.1.call-update
  8.0 0.0 all-gather.11.cloned.1.call-start
  8.1 0.7 all-gather.11.cloned.1.call-update
  8.7 0.0 all-gather.9.cloned.1.call-start
  8.8 0.0 copy-start.1
  8.8 3.2 %fusion = f32[512]{0:T(512)S(1)} fusion(bf16[512,4096]{1,0:T(8,128)(2,1)} %param.7), kind=kLoop, calls=%fused_computation.2 | loop fusion | flops 6290944 | bytes 4196352 | tf_op jit(solution)/shard_map/reduce_sum | solution.py:12
  12.0 0.0 copy-start.2
  12.1 0.0 copy-done
  12.1 0.0 copy-done.3
  12.1 0.2 copy-done.1
  12.2 3.4 %fusion.18 = f32[512,8]{0,1:T(8,128)S(1)} fusion(f32[4096,8]{0,1:T(8,128)S(1)} %copy-done, bf16[512,4096]{1,0:T(8,128)(2,1)S(1)} %copy-done.1, f32[4096]{0:T(1024)S(1)} %copy-done.3, f32[512]{0:T(512)S(1)} %add_rsqrt_fusion), kind=kOutput, calls=%fused_computation.16 | convolution fusion | flops 209727488 | bytes 4360192 | tf_op jit(solution)/shard_map/dot_general | solution.py:15
  15.7 0.0 copy-done.2
  15.7 42.8 %all-gather.5.cloned.1.call-done = bf16[2,4096,256]{2,1,0:T(8,128)(2,1)} async-done(((bf16[2,512,256]{2,1,0:T(8,128)(2,1)}), bf16[2,4096,256]{2,1,0:T(8,128)(2,1)}) %all-gather.5.cloned.1.call-update) | async-done | bytes 4194320 | tf_op jit(solution)/shard_map/all_gather | solution.py:24
  58.6 5.8 %fusion.5 = f32[512,2,256]{2,0,1:T(8,128)S(1)} fusion(bf16[2,4096,256]{2,1,0:T(8,128)(2,1)} %all-gather.5.cloned.1.call-done, bf16[512,4096]{1,0:T(8,128)(2,1)} %param.7, f32[4096]{0:T(1024)S(1)} %copy-done.3, f32[512]{0:T(512)S(1)} %add_rsqrt_fusion), kind=kOutput, calls=%fused_computation.7 | convolution fusion | flops 2155872256 | bytes 9455616 | tf_op jit(solution)/shard_map/td,edf->tef/dot_general | solution.py:28
  64.4 41.5 %all-gather.7.cloned.1.call-done = bf16[2,4096,256]{2,1,0:T(8,128)(2,1)} async-done(((bf16[2,512,256]{2,1,0:T(8,128)(2,1)}), bf16[2,4096,256]{2,1,0:T(8,128)(2,1)}) %all-gather.7.cloned.1.call-update) | async-done | bytes 4194320 | tf_op jit(solution)/shard_map/all_gather | solution.py:25
  105.9 6.8 %fusion.13 = bf16[512,2,256]{2,0,1:T(8,128)(2,1)} fusion(bf16[2,4096,256]{2,1,0:T(8,128)(2,1)} %all-gather.7.cloned.1.call-done, f32[512,2,256]{2,0,1:T(8,128)S(1)} %fusion.5, f32[512,2]{0,1:T(2,128)S(1)} %fusion.20, bf16[512,4096]{1,0:T(8,128)(2,1)} %param.7, f32[4096]{0:T(1024)S(1)} %copy-done.3, f32[512]{0:T(512)S(1)} %add_rsqrt_fusion), kind=kOutput, calls=%fused_computation.12 | convolution fusion | flops 2157707264 | bytes 9984000 | tf_op jit(solution)/shard_map/td,edf->tef/dot_general | solution.py:29
  112.6 0.0 all-gather.9.cloned.1.call-update
  112.7 40.5 %all-gather.11.cloned.1.call-done = bf16[2,1024,1024]{2,1,0:T(8,128)(2,1)} async-done(((bf16[2,128,1024]{2,1,0:T(8,128)(2,1)}), bf16[2,1024,1024]{2,1,0:T(8,128)(2,1)}) %all-gather.11.cloned.1.call-update) | async-done | bytes 4194320 | tf_op jit(solution)/shard_map/all_gather | solution.py:26
  153.2 35.6 %all-gather.9.cloned.1.call-done = bf16[512,2,1024]{2,0,1:T(8,128)(2,1)} async-done(((bf16[512,2,256]{2,0,1:T(8,128)(2,1)}), bf16[512,2,1024]{2,0,1:T(8,128)(2,1)}) %all-gather.9.cloned.1.call-update) | async-done | bytes 2097168 | tf_op jit(solution)/shard_map/all_gather | solution.py:31
  188.8 6.1 %bitcast_convert_fusion = bf16[512,1024]{1,0:T(8,128)(2,1)} fusion(bf16[512,2,1024]{2,0,1:T(8,128)(2,1)} %all-gather.9.cloned.1.call-done, bf16[2,1024,1024]{2,1,0:T(8,128)(2,1)} %all-gather.11.cloned.1.call-done), kind=kOutput, calls=%fused_computation.9 | convolution fusion | flops 2148007936 | bytes 7340032 | tf_op jit(solution)/shard_map/tef,efd->td/dot_general | solution.py:32
  (3 shorter events, 0.0 us)
Async XLA Ops:
  6.5 5.5 %copy-start = (f32[4096,8]{0,1:T(8,128)S(1)}, f32[4096,8]{0,1:T(8,128)}, u32[]{:S(2)}) copy-start(f32[4096,8]{0,1:T(8,128)} %param.9) | copy-start | bytes 393220
  6.5 5.5 %copy-start.3 = (f32[4096]{0:T(1024)S(1)}, f32[4096]{0:T(1024)}, u32[]{:S(2)}) copy-start(f32[4096]{0:T(1024)} %param.8) | copy-start | bytes 49156
  6.5 52.0 %all-gather.5.cloned.1.call-start = ((), (), s32[]{:S(2)}) async-start(), calls=%async_computation | async-start | bytes 4718592 | tf_op jit(solution)/shard_map/all_gather | solution.py:24
  7.3 98.6 %all-gather.7.cloned.1.call-start = ((), (), s32[]{:S(2)}) async-start(), calls=%async_computation.1 | async-start | bytes 4718592 | tf_op jit(solution)/shard_map/all_gather | solution.py:25
  8.0 145.2 %all-gather.11.cloned.1.call-start = ((), (), s32[]{:S(2)}) async-start(), calls=%async_computation.3 | async-start | bytes 4718592 | tf_op jit(solution)/shard_map/all_gather | solution.py:26
  8.7 180.0 %all-gather.9.cloned.1.call-start = ((), (), s32[]{:S(2)}) async-start(), calls=%async_computation.2 | async-start | bytes 2621440 | tf_op jit(solution)/shard_map/all_gather | solution.py:31
  8.8 3.5 %copy-start.1 = (bf16[512,4096]{1,0:T(8,128)(2,1)S(1)}, bf16[512,4096]{1,0:T(8,128)(2,1)}, u32[]{:S(2)}) copy-start(bf16[512,4096]{1,0:T(8,128)(2,1)} %param.7) | copy-start | bytes 12582916
  12.0 3.6 %copy-start.2 = (s32[512,2]{0,1:T(2,128)S(1)}, s32[512,2]{0,1:T(2,128)}, u32[]{:S(2)}) copy-start(s32[512,2]{0,1:T(2,128)} %param.10) | copy-start | bytes 12292
Sparse Core Ops, SparseCore 0:
  8.9 49.5 all-gather.4
  60.2 45.6 all-gather.6
  107.5 45.6 all-gather.10
  154.9 33.8 all-gather.8
where the time goes:
time: 202 us; the launch traced here: 201 us
  waiting for transfers between devices  162 us (80%)
  matrix products  22.2 us (11%)
  between operations  13.2 us (7%)
  other arithmetic  3.27 us (2%)
    all_gather x1, waiting for transfers between devices, per_device(): lax.all_gather(w_gate, 'dp', axis=1, tiled=True)  42.8 us
    all_gather x1, waiting for transfers between devices, per_device(): lax.all_gather(w_up, 'dp', axis=1, tiled=True)  41.5 us
    all_gather x1, waiting for transfers between devices, per_device(): lax.all_gather(w_down, 'dp', axis=1, tiled=True)  40.5 us
    all_gather x1, waiting for transfers between devices, per_device(): whole_hidden = lax.all_gather(hidden, 'tp', axis=2, tiled=True)  35.6 us
    dot_general x1, matrix products, per_device(): jnp.einsum('td,edf->tef', normed, full_up, preferred_element_type=jnp.flo...  6.76 us
    dot_general x1, matrix products, per_device(): jnp.einsum('tef,efd->td', whole_hidden, full_down, preferred_element_type...  6.12 us
    dot_general x1, matrix products, per_device(): jnp.einsum('td,edf->tef', normed, full_gate, preferred_element_type=jnp.f...  5.84 us
  transfers between devices with their start and end apart: 4, of which 4 were waited for; matrix products, arithmetic and copies ran while one was open for 10% of the time, Pallas kernels for 0%

commit v1 on v0

--- a/solution.py
+++ b/solution.py
@@ -5,6 +5,18 @@
 
 EPS = 1e-06
 ROUTE_SCALE = 2.5
+
+
+def summed_around(shard, axis, dim, term):
+    size, index, rows = (lax.axis_size(axis), lax.axis_index(axis), shard.shape[dim])
+    right = [(i, (i + 1) % size) for i in range(size)]
+    held, total = (shard, None)
+    for lap in range(size):
+        following = lax.ppermute(held, axis, right) if lap < size - 1 else None
+        update = term(held, (index - lap) % size * rows)
+        total = update if total is None else total + update
+        held = following
+    return total
 
 
 def per_device(tokens, gain, router, routes, w_gate, w_up, w_down):
@@ -28,8 +40,17 @@
     gate_value = jnp.einsum("td,edf->tef", normed, full_gate, preferred_element_type=jnp.float32)
     up_value = jnp.einsum("td,edf->tef", normed, full_up, preferred_element_type=jnp.float32)
     hidden = (jax.nn.silu(gate_value) * up_value * held_weights[:, :, None]).astype(jnp.bfloat16)
-    whole_hidden = lax.all_gather(hidden, "tp", axis=2, tiled=True)
-    mixed = jnp.einsum("tef,efd->td", whole_hidden, full_down, preferred_element_type=jnp.float32)
+    mixed = summed_around(
+        hidden,
+        "tp",
+        2,
+        lambda own_block, at: jnp.einsum(
+            "tef,efd->td",
+            own_block,
+            lax.dynamic_slice_in_dim(full_down, at, own_block.shape[2], axis=1),
+            preferred_element_type=jnp.float32,
+        ),
+    )
     return mixed.astype(jnp.bfloat16)
 
 

time: 202 us -> 179 us (0.89)
  waiting for transfers between devices: 162 us -> 138 us
  starting transfers between devices: 0.12 us -> 3.7 us
    all_gather x1 -> x0, waiting for transfers between devices: 35.6 us -> none  [per_device(): whole_hidden = lax.all_gather(hidden, 'tp', axis=2, tiled=True)]
    ppermute x0 -> x3, waiting for transfers between devices: none -> 25.5 us  [summed_around(): following = lax.ppermute(held, axis, right) if lap < size - 1 else None]
    all_gather x1, waiting for transfers between devices: 40.5 us -> 25.8 us  [per_device(): lax.all_gather(w_down, 'dp', axis=1, tiled=True)]
    ppermute x0 -> x3, starting transfers between devices: none -> 3.62 us  [summed_around(): following = lax.ppermute(held, axis, right) if lap < size - 1 else None]
    dot_general x1 -> x4, matrix products: 6.12 us -> 5.28 us  [per_device(): jnp.einsum('tef,efd->td', own_block, lax.dynamic_slice_in_dim(full_down,...]
  transfers between devices with their start and end apart: 4 -> 6, of which waited for: 4 -> 5; matrix products, arithmetic and copies ran while one was open for 10% -> 12% of each run, Pallas kernels for 0% -> 0%
where the time goes in v1:
time: 179 us
  waiting for transfers between devices  138 us (77%)
  matrix products  20.5 us (11%)
  between operations  13.2 us (7%)
  starting transfers between devices  3.7 us (2%)
  other arithmetic  3.27 us (2%)
    all_gather x1, waiting for transfers between devices, per_device(): lax.all_gather(w_gate, 'dp', axis=1, tiled=True)  42.9 us
    all_gather x1, waiting for transfers between devices, per_device(): lax.all_gather(w_up, 'dp', axis=1, tiled=True)  41.5 us
    all_gather x1, waiting for transfers between devices, per_device(): lax.all_gather(w_down, 'dp', axis=1, tiled=True)  25.8 us
    ppermute x3, waiting for transfers between devices, summed_around(): following = lax.ppermute(held, axis, right) if lap < size - 1 else None  25.5 us
    dot_general x1, matrix products, per_device(): jnp.einsum('td,edf->tef', normed, full_up, preferred_element_type=jnp.flo...  5.95 us
    dot_general x1, matrix products, per_device(): jnp.einsum('td,edf->tef', normed, full_gate, preferred_element_type=jnp.f...  5.84 us
    dot_general x4, matrix products, per_device(): jnp.einsum('tef,efd->td', own_block, lax.dynamic_slice_in_dim(full_down,...  5.28 us
    ppermute x3, starting transfers between devices, summed_around(): following = lax.ppermute(held, axis, right) if lap < size - 1 else None  3.62 us
  transfers between devices with their start and end apart: 6, of which 5 were waited for; matrix products, arithmetic and copies ran while one was open for 12% of the time, Pallas kernels for 0%

profile of v1, /device:TPU:0, one launch (start us, length us, event | category | flops | bytes accessed | tf_op | source)
XLA Modules:
  0.0 178.6 jit_solution(3672714353596637995)
XLA Ops:
  6.5 0.0 copy-start
  6.5 0.0 copy-start.4
  6.5 0.0 all-gather.4.cloned.1.call-start
  6.5 0.7 all-gather.4.cloned.1.call-update
  7.3 0.0 all-gather.6.cloned.1.call-start
  7.3 0.7 all-gather.6.cloned.1.call-update
  8.0 0.0 all-gather.8.cloned.1.call-start
  8.1 0.7 all-gather.8.cloned.1.call-update
  8.7 0.0 copy-start.2
  8.8 3.2 %fusion = f32[512]{0:T(512)S(1)} fusion(bf16[512,4096]{1,0:T(8,128)(2,1)} %param.7), kind=kLoop, calls=%fused_computation.2 | loop fusion | flops 6290944 | bytes 4196352 | tf_op jit(solution)/shard_map/reduce_sum | solution.py:24
  12.0 0.0 copy-start.3
  12.0 0.0 copy-done
  12.0 0.0 copy-done.4
  12.0 0.2 copy-done.2
  12.2 3.4 %fusion.19 = f32[512,8]{0,1:T(8,128)S(1)} fusion(f32[4096,8]{0,1:T(8,128)S(1)} %copy-done, bf16[512,4096]{1,0:T(8,128)(2,1)S(1)} %copy-done.2, f32[4096]{0:T(1024)S(1)} %copy-done.4, f32[512]{0:T(512)S(1)} %add_rsqrt_fusion), kind=kOutput, calls=%fused_computation.19 | convolution fusion | flops 209727488 | bytes 4360192 | tf_op jit(solution)/shard_map/dot_general | solution.py:27
  15.6 0.0 copy-done.3
  15.7 42.9 %all-gather.4.cloned.1.call-done = bf16[2,4096,256]{2,1,0:T(8,128)(2,1)} async-done(((bf16[2,512,256]{2,1,0:T(8,128)(2,1)}), bf16[2,4096,256]{2,1,0:T(8,128)(2,1)}) %all-gather.4.cloned.1.call-update) | async-done | bytes 4194320 | tf_op jit(solution)/shard_map/all_gather | solution.py:36
  58.6 5.8 %fusion.5 = f32[512,2,256]{2,0,1:T(8,128)S(1)} fusion(bf16[2,4096,256]{2,1,0:T(8,128)(2,1)} %all-gather.4.cloned.1.call-done, bf16[512,4096]{1,0:T(8,128)(2,1)} %param.7, f32[4096]{0:T(1024)S(1)} %copy-done.4, f32[512]{0:T(512)S(1)} %add_rsqrt_fusion), kind=kOutput, calls=%fused_computation.7 | convolution fusion | flops 2155872256 | bytes 9455616 | tf_op jit(solution)/shard_map/td,edf->tef/dot_general | solution.py:40
  64.4 41.5 %all-gather.6.cloned.1.call-done = bf16[2,4096,256]{2,1,0:T(8,128)(2,1)} async-done(((bf16[2,512,256]{2,1,0:T(8,128)(2,1)}), bf16[2,4096,256]{2,1,0:T(8,128)(2,1)}) %all-gather.6.cloned.1.call-update) | async-done | bytes 4194320 | tf_op jit(solution)/shard_map/all_gather | solution.py:37
  105.9 5.9 %fusion.14 = bf16[512,2,256]{2,0,1:T(8,128)(2,1)S(1)} fusion(bf16[2,4096,256]{2,1,0:T(8,128)(2,1)} %all-gather.6.cloned.1.call-done, f32[512,2,256]{2,0,1:T(8,128)S(1)} %fusion.5, f32[512,2]{0,1:T(2,128)S(1)} %fusion.28, bf16[512,4096]{1,0:T(8,128)(2,1)} %param.7, f32[4096]{0:T(1024)S(1)} %copy-done.4, f32[512]{0:T(512)S(1)} %add_rsqrt_fusion), kind=kOutput, calls=%fused_computation.15 | convolution fusion | flops 2157707264 | bytes 9984000 | tf_op jit(solution)/shard_map/td,edf->tef/dot_general | solution.py:41
  111.8 1.5 collective-permute-start
  113.4 13.5 %collective-permute-done = bf16[512,2,256]{2,0,1:T(8,128)(2,1)S(1)} collective-permute-done((bf16[512,2,256]{2,0,1:T(8,128)(2,1)S(1)}, bf16[512,2,256]{2,0,1:T(8,128)(2,1)S(1)}, u32[]{:S(2)}, u32[]{:S(2)}) %collective-permute-start) | collective-permute-done | bytes 524320 | tf_op jit(solution)/shard_map/ppermute | solution.py:15
  126.8 0.6 collective-permute-start.1
  127.4 25.8 %all-gather.8.cloned.1.call-done = bf16[2,1024,1024]{2,1,0:T(8,128)(2,1)} async-done(((bf16[2,128,1024]{2,1,0:T(8,128)(2,1)}), bf16[2,1024,1024]{2,1,0:T(8,128)(2,1)}) %all-gather.8.cloned.1.call-update) | async-done | bytes 4194320 | tf_op jit(solution)/shard_map/all_gather | solution.py:38
  153.2 0.0 copy-start.1
  153.2 2.1 %fusion.25 = f32[512,1024,1]{1,0,2:T(8,128)S(1)} fusion(bf16[512,2,256]{2,0,1:T(8,128)(2,1)S(1)} %fusion.14, bf16[2,1024,1024]{2,1,0:T(8,128)(2,1)} %all-gather.8.cloned.1.call-done, s32[]{:T(128)S(6)} %select_n.32), kind=kOutput, calls=%fused_computation.25 | convolution fusion | flops 536870912 | bytes 3670020 | tf_op jit(solution)/shard_map/tef,efd->td/dot_general | solution.py:47
  155.3 0.0 collective-permute-done.1
  155.3 1.5 collective-permute-start.2
  156.8 0.0 copy-done.1
  156.8 0.7 fusion.23
  157.5 0.7 fusion.21
  158.3 12.0 %collective-permute-done.2 = bf16[512,2,256]{2,0,1:T(8,128)(2,1)S(1)} collective-permute-done((bf16[512,2,256]{2,0,1:T(8,128)(2,1)S(1)}, bf16[512,2,256]{2,0,1:T(8,128)(2,1)S(1)}, u32[]{:S(2)}, u32[]{:S(2)}) %collective-permute-start.2) | collective-permute-done | bytes 524320 | tf_op jit(solution)/shard_map/ppermute | solution.py:15
  170.3 1.7 fusion.7
  (3 shorter events, 0.0 us)
Async XLA Ops:
  6.5 5.5 %copy-start = (f32[4096,8]{0,1:T(8,128)S(1)}, f32[4096,8]{0,1:T(8,128)}, u32[]{:S(2)}) copy-start(f32[4096,8]{0,1:T(8,128)} %param.9) | copy-start | bytes 393220
  6.5 5.5 %copy-start.4 = (f32[4096]{0:T(1024)S(1)}, f32[4096]{0:T(1024)}, u32[]{:S(2)}) copy-start(f32[4096]{0:T(1024)} %param.8) | copy-start | bytes 49156
  6.5 52.0 %all-gather.4.cloned.1.call-start = ((), (), s32[]{:S(2)}) async-start(), calls=%async_computation | async-start | bytes 4718592 | tf_op jit(solution)/shard_map/all_gather | solution.py:36
  7.3 98.6 %all-gather.6.cloned.1.call-start = ((), (), s32[]{:S(2)}) async-start(), calls=%async_computation.1 | async-start | bytes 4718592 | tf_op jit(solution)/shard_map/all_gather | solution.py:37
  8.0 145.2 %all-gather.8.cloned.1.call-start = ((), (), s32[]{:S(2)}) async-start(), calls=%async_computation.2 | async-start | bytes 4718592 | tf_op jit(solution)/shard_map/all_gather | solution.py:38
  8.7 3.5 %copy-start.2 = (bf16[512,4096]{1,0:T(8,128)(2,1)S(1)}, bf16[512,4096]{1,0:T(8,128)(2,1)}, u32[]{:S(2)}) copy-start(bf16[512,4096]{1,0:T(8,128)(2,1)} %param.7) | copy-start | bytes 12582916
  12.0 3.7 %copy-start.3 = (s32[512,2]{0,1:T(2,128)S(1)}, s32[512,2]{0,1:T(2,128)}, u32[]{:S(2)}) copy-start(s32[512,2]{0,1:T(2,128)} %param.10) | copy-start | bytes 12292
  111.8 15.0 %collective-permute-start = (bf16[512,2,256]{2,0,1:T(8,128)(2,1)S(1)}, bf16[512,2,256]{2,0,1:T(8,128)(2,1)S(1)}, u32[]{:S(2)}, u32[]{:S(2)}) collective-permute-start(bf16[512,2,256]{2,0,1:T(8,128)(2,1)S(1)} %fusion.14), channel_id=1, source_target_pairs={{0,1},{1,2},{2,3},{3,0},{4,5},{5,6},{6,7},{7,4},{8,9},{9,10},{10,1... | collective-permute-start | bytes 1572872 | tf_op jit(solution)/shard_map/ppermute | solution.py:15
  126.8 28.4 %collective-permute-start.1 = (bf16[512,2,256]{2,0,1:T(8,128)(2,1)S(1)}, bf16[512,2,256]{2,0,1:T(8,128)(2,1)S(1)}, u32[]{:S(2)}, u32[]{:S(2)}) collective-permute-start(bf16[512,2,256]{2,0,1:T(8,128)(2,1)S(1)} %collective-permute-done), channel_id=1, source_target_pairs={{0,1},{1,2},{2,3},{3,0},{4,5},{5,6},{6,7},{7,4},{8,9},{9,10},{10,1... | collective-permute-start | bytes 1572872 | tf_op jit(solution)/shard_map/ppermute | solution.py:15
  153.2 3.6 %copy-start.1 = (bf16[2,1024,1024]{2,1,0:T(8,128)(2,1)S(1)}, bf16[2,1024,1024]{2,1,0:T(8,128)(2,1)}, u32[]{:S(2)}) copy-start(bf16[2,1024,1024]{2,1,0:T(8,128)(2,1)} %all-gather.8.cloned.1.call-done) | copy-start | bytes 12582916
  155.3 15.0 %collective-permute-start.2 = (bf16[512,2,256]{2,0,1:T(8,128)(2,1)S(1)}, bf16[512,2,256]{2,0,1:T(8,128)(2,1)S(1)}, u32[]{:S(2)}, u32[]{:S(2)}) collective-permute-start(bf16[512,2,256]{2,0,1:T(8,128)(2,1)S(1)} %collective-permute-done.1), channel_id=1, source_target_pairs={{0,1},{1,2},{2,3},{3,0},{4,5},{5,6},{6,7},{7,4},{8,9},{9,10},{10,1... | collective-permute-start | bytes 1572872 | tf_op jit(solution)/shard_map/ppermute | solution.py:15
Sparse Core Ops, SparseCore 0:
  8.9 49.5 all-gather.3
  60.2 45.6 all-gather.5
  107.5 45.6 all-gather.7
